TPU v7x, 256 devices: a whole 4x4x8 slice. The times are simulated.
256 devices in a mesh: gx: 4 (over z_lo), gy: 8 (over z_hi, x), gz: 8 (over y, core).
Axes of the slice: x: 4, y: 4, z: 8 (z_hi: 2, z_lo: 4; z = z_hi * 4 + z_lo), core: 2. Of those that a mesh axis runs over, the one named last changes fastest.
Arguments:
- volume: bfloat16 [32, 8, 128, 1024], P(None, 'gx', 'gy', 'gz'), may hold values from -6 to 6
- w_first: bfloat16 [3, 3, 3, 32, 32], replicated, may hold values from -0.21875 to 0.21875
- w_second: bfloat16 [3, 3, 3, 32, 32], replicated, may hold values from -0.21875 to 0.21875
- v_first: bfloat16 [3, 3, 3, 32, 32], replicated, may hold values from -0.21875 to 0.21875
- v_second: bfloat16 [3, 3, 3, 32, 32], replicated, may hold values from -0.21875 to 0.21875
Outputs:
- jv: bfloat16 [32, 8, 128, 1024], P(None, 'gx', 'gy', 'gz')
- gv_first: float32 [3, 3, 3, 32, 32], replicated
- gv_second: float32 [3, 3, 3, 32, 32], replicated
All inputs are finite; a program needn't handle non-finite values.
Results may differ from a plain program's by a relative error of at most 0.005.
Values may be sent and summed in bfloat16 or wider, within the bound.
A program may use at most 64 MiB of HBM per device.

v0:
```python
import math
import jax
import jax.numpy as jnp
from jax import lax
from jax.sharding import PartitionSpec as P


def padded_2(cells, sides, width):
    for axis, dim in sides:
        count = lax.axis_size(axis)
        ends = count - 1
        head = lax.slice_in_dim(cells, 0, width, axis=dim)
        tail = lax.slice_in_dim(cells, cells.shape[dim] - width, cells.shape[dim], axis=dim)
        cells = jnp.concatenate(
            [
                lax.ppermute(tail, axis, [(i, (i + 1) % count) for i in range(ends)]),
                cells,
                lax.ppermute(head, axis, [((i + 1) % count, i) for i in range(ends)]),
            ],
            axis=dim,
        )
    return cells


def gelu_pair(pre):
    inner = 0.7978845608 * (pre + 0.044715 * pre * pre * pre)
    hyper = jnp.tanh(inner)
    hidden = 0.5 * pre * (1.0 + hyper)
    slope = 0.5 * (1.0 + hyper) + 0.5 * pre * (1.0 - hyper * hyper) * 0.7978845608 * (
        1.0 + 0.134145 * pre * pre
    )
    return (hidden, slope)


def stencil(padded, weight):
    depth = padded.shape[1] - 2
    height = padded.shape[2] - 2
    width = padded.shape[3] - 2
    in_chan = weight.shape[3]
    out_chan = weight.shape[4]
    summed = jnp.zeros((out_chan, depth, height, width), jnp.float32)
    for shift_x in range(3):
        for shift_y in range(3):
            stacked = jnp.concatenate(
                [
                    padded[
                        :,
                        shift_x : shift_x + depth,
                        shift_y : shift_y + height,
                        shift_z : shift_z + width,
                    ]
                    for shift_z in range(3)
                ],
                axis=0,
            )
            matrix = weight[shift_x, shift_y].reshape(3 * in_chan, out_chan)
            summed = summed + jnp.einsum(
                "kxyz,ko->oxyz", stacked, matrix, preferred_element_type=jnp.float32
            )
    return summed


def correlate(padded, target):
    depth = target.shape[1]
    height = target.shape[2]
    width = target.shape[3]
    in_chan = padded.shape[0]
    out_chan = target.shape[0]
    planes = []
    for shift_x in range(3):
        rows_y = []
        for shift_y in range(3):
            stacked = jnp.concatenate(
                [
                    padded[
                        :,
                        shift_x : shift_x + depth,
                        shift_y : shift_y + height,
                        shift_z : shift_z + width,
                    ]
                    for shift_z in range(3)
                ],
                axis=0,
            )
            product = jnp.einsum(
                "kxyz,oxyz->ko", stacked, target, preferred_element_type=jnp.float32
            )
            rows_y.append(product.reshape(3, in_chan, out_chan))
        planes.append(jnp.stack(rows_y))
    return jnp.stack(planes)


def body(volume, w_first, w_second, v_first, v_second):
    channels = volume.shape[0]
    depth = volume.shape[1]
    height = volume.shape[2]
    width = volume.shape[3]
    count_all = float(
        depth * height * width * lax.axis_size("gx") * lax.axis_size("gy") * lax.axis_size("gz")
    )
    factor = math.sqrt(27.0 * channels)
    input_pad = padded_2(volume, (("gx", 1), ("gy", 2), ("gz", 3)), 1)
    pre = stencil(input_pad, w_first)
    hidden_f, slope = gelu_pair(pre)
    hidden = hidden_f.astype(jnp.bfloat16)
    tangent = (slope * stencil(input_pad, v_first)).astype(jnp.bfloat16)
    paired = padded_2(jnp.stack([hidden, tangent]), (("gx", 2), ("gy", 3), ("gz", 4)), 1)
    hidden_pad = paired[0]
    tangent_pad = paired[1]
    jv = (stencil(tangent_pad, w_second) + stencil(hidden_pad, v_second)).astype(jnp.bfloat16)
    local_second = correlate(hidden_pad, jv)
    jv_pad = padded_2(jv, (("gx", 1), ("gy", 2), ("gz", 3)), 1)
    flipped = jnp.transpose(jnp.flip(w_second, (0, 1, 2)), (0, 1, 2, 4, 3))
    back = (slope * stencil(jv_pad, flipped)).astype(jnp.bfloat16)
    local_first = correlate(input_pad, back)
    summed_first, summed_second = lax.psum((local_first, local_second), ("gx", "gy", "gz"))
    gv_first = factor * (summed_first / count_all + 0.1 * v_first.astype(jnp.float32))
    gv_second = factor * (summed_second / count_all + 0.1 * v_second.astype(jnp.float32))
    return (jv, gv_first, gv_second)


def solution(mesh):
    in_specs = (P(None, "gx", "gy", "gz"), P(), P(), P(), P())
    out_specs = (P(None, "gx", "gy", "gz"), P(), P())
    return jax.shard_map(body, mesh=mesh, in_specs=in_specs, out_specs=out_specs, check_vma=False)
```

profile of v0, /device:TPU:2, one launch (start us, length us, event | category | flops | bytes accessed | tf_op | source)
XLA Modules:
  0.0 443.7 jit_solution(16340484945520998631)
XLA Ops:
  8.4 1.3 collective-permute-start.1
  9.7 4.6 %collective-permute-start = (bf16[32,1,16,128]{3,0,2,1:T(8,128)(2,1)S(1)}, bf16[32,1,16,128]{3,0,2,1:T(8,128)(2,1)S(1)}, u32[]{:S(2)}, u32[]{:S(2)}) collective-permute-start(bf16[32,1,16,128]{3,0,2,1:T(8,128)(2,1)S(1)} %get-tuple-element.141), channel_id=1, source_target_pairs={{0,64},{64,128},{128,192},{1,65},{65,129},{129,193},{2,66},{66,130... | collective-permute-start | bytes 393224 | tf_op jit(solution)/shard_map/ppermute | solution.py:16
  14.2 1.5 fusion.203
  17.1 3.4 collective-permute-start.2
  20.5 2.4 collective-permute-start.3
  23.6 2.7 collective-permute-done.3
  28.2 1.3 collective-permute-start.5
  29.5 3.0 collective-permute-start.4
  45.1 4.4 collective-permute-start.6
  49.5 1.3 collective-permute-start.7
  51.6 4.3 collective-permute-done.6
  55.9 4.5 %collective-permute-done.7 = bf16[2,32,1,16,128]{4,1,3,2,0:T(8,128)(2,1)S(1)} collective-permute-done((bf16[2,32,1,16,128]{4,1,3,2,0:T(8,128)(2,1)S(1)}, bf16[2,32,1,16,128]{4,1,3,2,0:T(8,128)(2,1)S(1)}, u32[]{:S(2)}, u32[]{:S(2)}) %collective-permute-start.7) | collective-permute-done | bytes 262176 | tf_op jit(solution)/shard_map/ppermute | solution.py:18
  60.5 8.2 %collective-permute-start.8 = (bf16[2,32,4,1,128]{4,1,3,2,0:T(8,128)(2,1)S(1)}, bf16[2,32,4,1,128]{4,1,3,2,0:T(8,128)(2,1)S(1)}, u32[]{:S(2)}, u32[]{:S(2)}) collective-permute-start(bf16[2,32,4,1,128]{4,1,3,2,0:T(8,128)(2,1)S(1)} %get-tuple-element.108), channel_id=1, source_target_pairs={{0,8},{8,16},{16,24},{24,32},{32,40},{40,48},{48,56},{1,9},{9,17},... | collective-permute-start | bytes 196616 | tf_op jit(solution)/shard_map/ppermute | solution.py:16
  68.7 1.9 collective-permute-start.9
  71.3 9.5 %collective-permute-done.9 = bf16[2,32,4,1,128]{4,1,3,2,0:T(8,128)(2,1)S(1)} collective-permute-done((bf16[2,32,4,1,128]{4,1,3,2,0:T(8,128)(2,1)S(1)}, bf16[2,32,4,1,128]{4,1,3,2,0:T(8,128)(2,1)S(1)}, u32[]{:S(2)}, u32[]{:S(2)}) %collective-permute-start.9) | collective-permute-done | bytes 65568 | tf_op jit(solution)/shard_map/ppermute | solution.py:18
  82.3 1.5 copy.162
  84.8 1.3 collective-permute-start.11
  86.1 3.2 collective-permute-start.10
  89.3 1.6 fusion.201
  97.1 1.7 copy.165
  98.8 3.8 pad_maximum_fusion
  117.3 2.9 collective-permute-start.12
  120.3 1.3 collective-permute-start.13
  122.0 1.9 collective-permute-done.12
  123.9 4.5 %collective-permute-done.13 = bf16[32,1,16,128]{3,0,2,1:T(8,128)(2,1)S(1)} collective-permute-done((bf16[32,1,16,128]{3,0,2,1:T(8,128)(2,1)S(1)}, bf16[32,1,16,128]{3,0,2,1:T(8,128)(2,1)S(1)}, u32[]{:S(2)}, u32[]{:S(2)}) %collective-permute-start.13) | collective-permute-done | bytes 131104 | tf_op jit(solution)/shard_map/ppermute | solution.py:18
  128.5 3.9 collective-permute-start.14
  132.4 2.1 collective-permute-start.15
  135.6 7.3 %collective-permute-done.15 = bf16[32,4,1,128]{3,0,2,1:T(8,128)(2,1)S(1)} collective-permute-done((bf16[32,4,1,128]{3,0,2,1:T(8,128)(2,1)S(1)}, bf16[32,4,1,128]{3,0,2,1:T(8,128)(2,1)S(1)}, u32[]{:S(2)}, u32[]{:S(2)}) %collective-permute-start.15) | collective-permute-done | bytes 32800 | tf_op jit(solution)/shard_map/ppermute | solution.py:18
  145.5 3.0 collective-permute-start.16
  150.8 1.4 maximum_maximum_fusion.1
  170.5 262.7 %all-reduce.3.cloned.1.call-done = (f32[3,3,3,32,32]{3,2,4,1,0:T(4,128)}, f32[3,3,3,32,32]{3,2,4,1,0:T(4,128)}) async-done(((f32[3,3,3,32,32]{3,2,4,1,0:T(4,128)}, f32[3,3,3,32,32]{3,2,4,1,0:T(4,128)}), (f32[3,3,3,32,32]{3,2,4,1,0:T(4,128)}, f32[3,3,3,32,32]{3,2,4,1,0:T(4,128)})) %all-reduce.3.cloned.1.call-update) | async-done | bytes 221200 | tf_op jit(solution)/shard_map/psum | solution.py:116
  433.2 1.4 add_multiply_fusion.1
  (385 shorter events, 67.8 us)
Async XLA Ops:
  7.2 9.7 %copy-start.2 = (bf16[32,2,16,128]{3,2,1,0:T(8,128)(2,1)S(1)}, bf16[32,2,16,128]{3,2,1,0:T(8,128)(2,1)}, u32[]{:S(2)}) copy-start(bf16[32,2,16,128]{3,2,1,0:T(8,128)(2,1)} %param.5) | copy-start | bytes 786436
  7.2 15.8 %copy-start.6 = (bf16[3,3,3,32,32]{4,3,2,1,0:T(8,128)(2,1)S(1)}, bf16[3,3,3,32,32]{4,3,2,1,0:T(8,128)(2,1)}, u32[]{:S(2)}) copy-start(bf16[3,3,3,32,32]{4,3,2,1,0:T(8,128)(2,1)} %param.8) | copy-start | bytes 165892
  7.2 426.0 %all-reduce.3.cloned.1.call-start = ((), (), s32[]{:S(2)}) async-start(), calls=%async_computation | async-start | bytes 2359296 | tf_op jit(solution)/shard_map/psum | solution.py:116
  8.3 35.9 %copy-start.3 = (bf16[32,2,16,128]{3,0,2,1:T(8,128)(2,1)}, bf16[32,2,16,128]{3,0,2,1:T(8,128)(2,1)S(1)}, u32[]{:S(2)}) copy-start(bf16[32,2,16,128]{3,0,2,1:T(8,128)(2,1)S(1)} %copy.134) | copy-start | bytes 786436
  8.4 8.6 %collective-permute-start.1 = (bf16[32,1,16,128]{3,0,2,1:T(8,128)(2,1)S(1)}, bf16[32,1,16,128]{3,0,2,1:T(8,128)(2,1)S(1)}, u32[]{:S(2)}, u32[]{:S(2)}) collective-permute-start(bf16[32,1,16,128]{3,0,2,1:T(8,128)(2,1)S(1)} %get-tuple-element.140), channel_id=1, source_target_pairs={{64,0},{128,64},{192,128},{65,1},{129,65},{193,129},{66,2},{130,66... | collective-permute-start | bytes 393224 | tf_op jit(solution)/shard_map/ppermute | solution.py:18
  9.7 7.2 %collective-permute-start = (bf16[32,1,16,128]{3,0,2,1:T(8,128)(2,1)S(1)}, bf16[32,1,16,128]{3,0,2,1:T(8,128)(2,1)S(1)}, u32[]{:S(2)}, u32[]{:S(2)}) collective-permute-start(bf16[32,1,16,128]{3,0,2,1:T(8,128)(2,1)S(1)} %get-tuple-element.141), channel_id=1, source_target_pairs={{0,64},{64,128},{128,192},{1,65},{65,129},{129,193},{2,66},{66,130... | collective-permute-start | bytes 393224 | tf_op jit(solution)/shard_map/ppermute | solution.py:16
  16.9 24.9 %copy-start.61 = (bf16[32,1,16,128]{3,0,2,1:T(8,128)(2,1)}, bf16[32,1,16,128]{3,0,2,1:T(8,128)(2,1)S(1)}, u32[]{:S(2)}) copy-start(bf16[32,1,16,128]{3,0,2,1:T(8,128)(2,1)S(1)} %collective-permute-done) | copy-start | bytes 393220
  17.0 27.2 %copy-start.59 = (bf16[32,1,16,128]{3,0,2,1:T(8,128)(2,1)}, bf16[32,1,16,128]{3,0,2,1:T(8,128)(2,1)S(1)}, u32[]{:S(2)}) copy-start(bf16[32,1,16,128]{3,0,2,1:T(8,128)(2,1)S(1)} %collective-permute-done.1) | copy-start | bytes 393220
  17.1 6.5 %collective-permute-start.2 = (bf16[32,4,1,128]{3,0,2,1:T(8,128)(2,1)S(1)}, bf16[32,4,1,128]{3,0,2,1:T(8,128)(2,1)S(1)}, u32[]{:S(2)}, u32[]{:S(2)}) collective-permute-start(bf16[32,4,1,128]{3,0,2,1:T(8,128)(2,1)S(1)} %get-tuple-element.136), channel_id=1, source_target_pairs={{0,8},{8,16},{16,24},{24,32},{32,40},{40,48},{48,56},{1,9},{9,17},... | collective-permute-start | bytes 98312 | tf_op jit(solution)/shard_map/ppermute | solution.py:16
  20.5 5.8 %collective-permute-start.3 = (bf16[32,4,1,128]{3,0,2,1:T(8,128)(2,1)S(1)}, bf16[32,4,1,128]{3,0,2,1:T(8,128)(2,1)S(1)}, u32[]{:S(2)}, u32[]{:S(2)}) collective-permute-start(bf16[32,4,1,128]{3,0,2,1:T(8,128)(2,1)S(1)} %get-tuple-element.137), channel_id=1, source_target_pairs={{8,0},{16,8},{24,16},{32,24},{40,32},{48,40},{56,48},{9,1},{17,9},... | collective-permute-start | bytes 98312 | tf_op jit(solution)/shard_map/ppermute | solution.py:18
  28.2 5.9 %collective-permute-start.5 = (bf16[32,4,18,1]{0,1,3,2:T(4,128)(2,1)S(1)}, bf16[32,4,18,1]{0,1,3,2:T(4,128)(2,1)}, u32[]{:S(2)}, u32[]{:S(2)}) collective-permute-start(bf16[32,4,18,1]{0,1,3,2:T(4,128)(2,1)S(1)} %copy.139), channel_id=1, source_target_pairs={{1,0},{2,1},{3,2},{4,3},{5,4},{6,5},{7,6},{9,8},{10,9},{11,10},{12... | collective-permute-start | bytes 13832 | tf_op jit(solution)/shard_map/ppermute | solution.py:18
  29.5 4.1 collective-permute-start.4
  32.7 9.5 %copy-start.15 = (bf16[32,2,16,128]{3,0,2,1:T(8,128)(2,1)}, bf16[32,2,16,128]{3,0,2,1:T(8,128)(2,1)S(1)}, u32[]{:S(2)}) copy-start(bf16[32,2,16,128]{3,0,2,1:T(8,128)(2,1)S(1)} %get-tuple-element.125) | copy-start | bytes 786436
  32.7 10.2 %copy-start.17 = (bf16[32,2,16,128]{3,0,2,1:T(8,128)(2,1)}, bf16[32,2,16,128]{3,0,2,1:T(8,128)(2,1)S(1)}, u32[]{:S(2)}) copy-start(bf16[32,2,16,128]{3,0,2,1:T(8,128)(2,1)S(1)} %get-tuple-element.135) | copy-start | bytes 786436
  32.7 10.9 %copy-start.23 = (bf16[32,2,16,128]{3,0,2,1:T(8,128)(2,1)}, bf16[32,2,16,128]{3,0,2,1:T(8,128)(2,1)S(1)}, u32[]{:S(2)}) copy-start(bf16[32,2,16,128]{3,0,2,1:T(8,128)(2,1)S(1)} %get-tuple-element.124) | copy-start | bytes 786436
  45.1 10.8 %collective-permute-start.6 = (bf16[2,32,1,16,128]{4,1,3,2,0:T(8,128)(2,1)S(1)}, bf16[2,32,1,16,128]{4,1,3,2,0:T(8,128)(2,1)S(1)}, u32[]{:S(2)}, u32[]{:S(2)}) collective-permute-start(bf16[2,32,1,16,128]{4,1,3,2,0:T(8,128)(2,1)S(1)} %get-tuple-element.132), channel_id=1, source_target_pairs={{0,64},{64,128},{128,192},{1,65},{65,129},{129,193},{2,66},{66,130... | collective-permute-start | bytes 786440 | tf_op jit(solution)/shard_map/ppermute | solution.py:16
  49.5 10.9 %collective-permute-start.7 = (bf16[2,32,1,16,128]{4,1,3,2,0:T(8,128)(2,1)S(1)}, bf16[2,32,1,16,128]{4,1,3,2,0:T(8,128)(2,1)S(1)}, u32[]{:S(2)}, u32[]{:S(2)}) collective-permute-start(bf16[2,32,1,16,128]{4,1,3,2,0:T(8,128)(2,1)S(1)} %get-tuple-element.133), channel_id=1, source_target_pairs={{64,0},{128,64},{192,128},{65,1},{129,65},{193,129},{66,2},{130,66... | collective-permute-start | bytes 786440 | tf_op jit(solution)/shard_map/ppermute | solution.py:18
  55.9 24.9 %copy-start = (bf16[2,32,1,16,128]{4,1,3,2,0:T(8,128)(2,1)}, bf16[2,32,1,16,128]{4,1,3,2,0:T(8,128)(2,1)S(1)}, u32[]{:S(2)}) copy-start(bf16[2,32,1,16,128]{4,1,3,2,0:T(8,128)(2,1)S(1)} %collective-permute-done.6) | copy-start | bytes 786436
  60.5 20.4 %copy-start.1 = (bf16[2,32,1,16,128]{4,1,3,2,0:T(8,128)(2,1)}, bf16[2,32,1,16,128]{4,1,3,2,0:T(8,128)(2,1)S(1)}, u32[]{:S(2)}) copy-start(bf16[2,32,1,16,128]{4,1,3,2,0:T(8,128)(2,1)S(1)} %collective-permute-done.7) | copy-start | bytes 786436
  60.5 10.8 %collective-permute-start.8 = (bf16[2,32,4,1,128]{4,1,3,2,0:T(8,128)(2,1)S(1)}, bf16[2,32,4,1,128]{4,1,3,2,0:T(8,128)(2,1)S(1)}, u32[]{:S(2)}, u32[]{:S(2)}) collective-permute-start(bf16[2,32,4,1,128]{4,1,3,2,0:T(8,128)(2,1)S(1)} %get-tuple-element.108), channel_id=1, source_target_pairs={{0,8},{8,16},{16,24},{24,32},{32,40},{40,48},{48,56},{1,9},{9,17},... | collective-permute-start | bytes 196616 | tf_op jit(solution)/shard_map/ppermute | solution.py:16
  68.7 12.2 %collective-permute-start.9 = (bf16[2,32,4,1,128]{4,1,3,2,0:T(8,128)(2,1)S(1)}, bf16[2,32,4,1,128]{4,1,3,2,0:T(8,128)(2,1)S(1)}, u32[]{:S(2)}, u32[]{:S(2)}) collective-permute-start(bf16[2,32,4,1,128]{4,1,3,2,0:T(8,128)(2,1)S(1)} %get-tuple-element.109), channel_id=1, source_target_pairs={{8,0},{16,8},{24,16},{32,24},{40,32},{48,40},{56,48},{9,1},{17,9},... | collective-permute-start | bytes 196616 | tf_op jit(solution)/shard_map/ppermute | solution.py:18
  83.8 10.1 %copy-start.66 = (bf16[1,1,3,32,32]{3,4,2,1,0:T(8,128)(2,1)S(1)}, bf16[1,1,3,32,32]{3,4,2,1,0:T(8,128)(2,1)}, u32[]{:S(2)}) copy-start(bf16[1,1,3,32,32]{3,4,2,1,0:T(8,128)(2,1)} %get-tuple-element.148) | copy-start | bytes 18436
  83.8 10.8 %copy-start.65 = (bf16[1,1,3,32,32]{3,4,2,1,0:T(8,128)(2,1)S(1)}, bf16[1,1,3,32,32]{3,4,2,1,0:T(8,128)(2,1)}, u32[]{:S(2)}) copy-start(bf16[1,1,3,32,32]{3,4,2,1,0:T(8,128)(2,1)} %get-tuple-element.149) | copy-start | bytes 18436
  83.8 11.5 %copy-start.64 = (bf16[1,1,3,32,32]{3,4,2,1,0:T(8,128)(2,1)S(1)}, bf16[1,1,3,32,32]{3,4,2,1,0:T(8,128)(2,1)}, u32[]{:S(2)}) copy-start(bf16[1,1,3,32,32]{3,4,2,1,0:T(8,128)(2,1)} %get-tuple-element.150) | copy-start | bytes 18436
  84.8 12.3 %collective-permute-start.11 = (bf16[2,32,4,18,1]{1,2,4,3,0:T(4,128)(2,1)S(1)}, bf16[2,32,4,18,1]{1,2,4,3,0:T(4,128)(2,1)}, u32[]{:S(2)}, u32[]{:S(2)}) collective-permute-start(bf16[2,32,4,18,1]{1,2,4,3,0:T(4,128)(2,1)S(1)} %copy.163), channel_id=1, source_target_pairs={{1,0},{2,1},{3,2},{4,3},{5,4},{6,5},{7,6},{9,8},{10,9},{11,10},{12... | collective-permute-start | bytes 27656 | tf_op jit(solution)/shard_map/ppermute | solution.py:18
  86.1 10.0 %collective-permute-start.10 = (bf16[2,32,4,18,1]{1,2,4,3,0:T(4,128)(2,1)}, bf16[2,32,4,18,1]{1,2,4,3,0:T(4,128)(2,1)S(1)}, u32[]{:S(2)}, u32[]{:S(2)}) collective-permute-start(bf16[2,32,4,18,1]{1,2,4,3,0:T(4,128)(2,1)} %copy.162), channel_id=1, source_target_pairs={{0,1},{1,2},{2,3},{3,4},{4,5},{5,6},{6,7},{8,9},{9,10},{10,11},{11... | collective-permute-start | bytes 27656 | tf_op jit(solution)/shard_map/ppermute | solution.py:16
  117.3 6.6 %collective-permute-start.12 = (bf16[32,1,16,128]{3,0,2,1:T(8,128)(2,1)S(1)}, bf16[32,1,16,128]{3,0,2,1:T(8,128)(2,1)S(1)}, u32[]{:S(2)}, u32[]{:S(2)}) collective-permute-start(bf16[32,1,16,128]{3,0,2,1:T(8,128)(2,1)S(1)} %get-tuple-element.138), channel_id=1, source_target_pairs={{0,64},{64,128},{128,192},{1,65},{65,129},{129,193},{2,66},{66,130... | collective-permute-start | bytes 393224 | tf_op jit(solution)/shard_map/ppermute | solution.py:16
  120.3 8.2 %collective-permute-start.13 = (bf16[32,1,16,128]{3,0,2,1:T(8,128)(2,1)S(1)}, bf16[32,1,16,128]{3,0,2,1:T(8,128)(2,1)S(1)}, u32[]{:S(2)}, u32[]{:S(2)}) collective-permute-start(bf16[32,1,16,128]{3,0,2,1:T(8,128)(2,1)S(1)} %get-tuple-element.139), channel_id=1, source_target_pairs={{64,0},{128,64},{192,128},{65,1},{129,65},{193,129},{66,2},{130,66... | collective-permute-start | bytes 393224 | tf_op jit(solution)/shard_map/ppermute | solution.py:18
  128.5 7.1 %collective-permute-start.14 = (bf16[32,4,1,128]{3,0,2,1:T(8,128)(2,1)S(1)}, bf16[32,4,1,128]{3,0,2,1:T(8,128)(2,1)S(1)}, u32[]{:S(2)}, u32[]{:S(2)}) collective-permute-start(bf16[32,4,1,128]{3,0,2,1:T(8,128)(2,1)S(1)} %get-tuple-element.130), channel_id=1, source_target_pairs={{0,8},{8,16},{16,24},{24,32},{32,40},{40,48},{48,56},{1,9},{9,17},... | collective-permute-start | bytes 98312 | tf_op jit(solution)/shard_map/ppermute | solution.py:16
  132.4 10.5 %collective-permute-start.15 = (bf16[32,4,1,128]{3,0,2,1:T(8,128)(2,1)S(1)}, bf16[32,4,1,128]{3,0,2,1:T(8,128)(2,1)S(1)}, u32[]{:S(2)}, u32[]{:S(2)}) collective-permute-start(bf16[32,4,1,128]{3,0,2,1:T(8,128)(2,1)S(1)} %get-tuple-element.131), channel_id=1, source_target_pairs={{8,0},{16,8},{24,16},{32,24},{40,32},{48,40},{56,48},{9,1},{17,9},... | collective-permute-start | bytes 98312 | tf_op jit(solution)/shard_map/ppermute | solution.py:18
  144.2 6.0 %collective-permute-start.17 = (bf16[32,4,18,1]{0,1,3,2:T(4,128)(2,1)S(1)}, bf16[32,4,18,1]{0,1,3,2:T(4,128)(2,1)S(1)}, u32[]{:S(2)}, u32[]{:S(2)}) collective-permute-start(bf16[32,4,18,1]{0,1,3,2:T(4,128)(2,1)S(1)} %copy.186), channel_id=1, source_target_pairs={{1,0},{2,1},{3,2},{4,3},{5,4},{6,5},{7,6},{9,8},{10,9},{11,10},{12... | collective-permute-start | bytes 13832 | tf_op jit(solution)/shard_map/ppermute | solution.py:18
  145.5 4.2 collective-permute-start.16
  (94 other events, 229.5 us)
Sparse Core Ops, SparseCore 0:
  169.4 263.7 all-reduce.2
where the time goes:
time: 446 us; the launch traced here: 444 us
  waiting for transfers between devices  300 us (67%)
  starting transfers between devices  51 us (11%)
  local copies, waits for them, and re-layouts  47.2 us (11%)
  matrix products  19.3 us (4%)
  between operations  15.8 us (4%)
  other arithmetic  10.9 us (2%)
    psum x1, waiting for transfers between devices, body(): lax.psum((local_first, local_second), ('gx', 'gy', 'gz'))  263 us
    ppermute x9, starting transfers between devices, padded_2(): lax.ppermute(tail, axis, [(i, (i + 1) % count) for i in range(ends)])  36.7 us
    ppermute x9, waiting for transfers between devices, padded_2(): lax.ppermute(head, axis, [((i + 1) % count, i) for i in range(ends)])  28.6 us
    unnamed x222, local copies, waits for them, and re-layouts  16.6 us
    ppermute x9, starting transfers between devices, padded_2(): lax.ppermute(head, axis, [((i + 1) % count, i) for i in range(ends)])  14.2 us
    dot_general x45, matrix products, stencil(): jnp.einsum('kxyz,ko->oxyz', stacked, matrix, preferred_element_type=jnp.f...  12.7 us
  transfers between devices with their start and end apart: 19, of which 10 were waited for; matrix products, arithmetic and copies ran while one was open for 4% of the time, Pallas kernels for 0%

commit v1 on v0

--- a/solution.py
+++ b/solution.py
@@ -1,8 +1,18 @@
+import functools
 import math
 import jax
 import jax.numpy as jnp
 from jax import lax
 from jax.sharding import PartitionSpec as P
+from jax.lax import psum
+
+
+def unite_sections(block_here, peer_axis, named_axis):
+    f_next = psum(block_here, peer_axis)
+    return psum(f_next, named_axis)
+
+
+supply_digits = functools.partial(unite_sections, peer_axis="gx", named_axis=("gy", "gz"))
 
 
 def padded_2(cells, sides, width):
@@ -113,7 +123,7 @@
     flipped = jnp.transpose(jnp.flip(w_second, (0, 1, 2)), (0, 1, 2, 4, 3))
     back = (slope * stencil(jv_pad, flipped)).astype(jnp.bfloat16)
     local_first = correlate(input_pad, back)
-    summed_first, summed_second = lax.psum((local_first, local_second), ("gx", "gy", "gz"))
+    summed_first, summed_second = supply_digits((local_first, local_second))
     gv_first = factor * (summed_first / count_all + 0.1 * v_first.astype(jnp.float32))
     gv_second = factor * (summed_second / count_all + 0.1 * v_second.astype(jnp.float32))
     return (jv, gv_first, gv_second)

time: 446 us -> 1020 us (2.29)
  the two profiles are of different devices: /device:TPU:2 before, /device:TPU:32 now
where the time goes in v1:
time: 1020 us
  waiting for transfers between devices  878 us (86%)
  starting transfers between devices  50 us (5%)
  local copies, waits for them, and re-layouts  47.2 us (5%)
  matrix products  19.3 us (2%)
  between operations  15.8 us (2%)
  other arithmetic  10.9 us (1%)
    psum x1, waiting for transfers between devices, unite_sections(): return psum(f_next, named_axis)  772 us
    psum x1, waiting for transfers between devices, unite_sections(): f_next = psum(block_here, peer_axis)  74.3 us
    ppermute x9, starting transfers between devices, padded_2(): lax.ppermute(tail, axis, [(i, (i + 1) % count) for i in range(ends)])  33.3 us
    ppermute x9, waiting for transfers between devices, padded_2(): lax.ppermute(head, axis, [((i + 1) % count, i) for i in range(ends)])  21.7 us
  transfers between devices with their start and end apart: 20, of which 11 were waited for; matrix products, arithmetic and copies ran while one was open for 2% of the time, Pallas kernels for 0%

profile of v1, /device:TPU:32, one launch (start us, length us, event | category | flops | bytes accessed | tf_op | source)
XLA Modules:
  0.0 1021.6 jit_solution(3891689551164280670)
XLA Ops:
  8.4 3.7 collective-permute-start.1
  12.1 2.1 collective-permute-start
  14.2 1.5 fusion.203
  15.7 3.2 collective-permute-done
  19.2 1.9 collective-permute-start.2
  21.0 1.3 collective-permute-start.3
  23.0 3.8 collective-permute-done.3
  30.1 3.0 collective-permute-start.4
  45.7 3.8 collective-permute-start.6
  49.5 2.0 collective-permute-start.7
  52.3 4.2 collective-permute-done.6
  56.5 4.1 collective-permute-done.7
  60.6 3.4 collective-permute-start.8
  64.0 1.3 collective-permute-start.9
  66.1 7.3 collective-permute-done.9
  74.8 1.5 copy.162
  78.6 3.2 collective-permute-start.10
  81.9 1.6 fusion.201
  89.6 1.7 copy.165
  91.3 3.8 pad_maximum_fusion
  109.9 2.9 collective-permute-start.12
  112.8 2.9 collective-permute-start.13
  116.2 1.7 collective-permute-done.12
  117.9 3.1 collective-permute-done.13
  121.0 9.9 collective-permute-start.14
  131.0 1.5 collective-permute-start.15
  133.5 3.3 collective-permute-done.15
  139.4 3.0 collective-permute-start.16
  144.7 1.4 maximum_maximum_fusion.1
  163.2 74.3 %all-reduce.7.cloned.1.call-done = (f32[3,3,3,32,32]{3,2,4,1,0:T(4,128)}, f32[3,3,3,32,32]{3,2,4,1,0:T(4,128)}) async-done(((f32[3,3,3,32,32]{3,2,4,1,0:T(4,128)}, f32[3,3,3,32,32]{3,2,4,1,0:T(4,128)}), (f32[3,3,3,32,32]{3,2,4,1,0:T(4,128)}, f32[3,3,3,32,32]{3,2,4,1,0:T(4,128)})) %all-reduce.7.cloned.1.call-update) | async-done | bytes 221200 | tf_op jit(solution)/shard_map/psum | solution.py:11
  238.8 772.3 %all-reduce.5.cloned.1.call-done = (f32[3,3,3,32,32]{3,2,4,1,0:T(4,128)}, f32[3,3,3,32,32]{3,2,4,1,0:T(4,128)}) async-done(((f32[3,3,3,32,32]{3,2,4,1,0:T(4,128)}, f32[3,3,3,32,32]{3,2,4,1,0:T(4,128)}), (f32[3,3,3,32,32]{3,2,4,1,0:T(4,128)}, f32[3,3,3,32,32]{3,2,4,1,0:T(4,128)})) %all-reduce.5.cloned.1.call-update) | async-done | bytes 221200 | tf_op jit(solution)/shard_map/psum | solution.py:12
  1011.1 1.4 add_multiply_fusion.1
  (388 shorter events, 69.3 us)
Async XLA Ops:
  7.2 11.8 %copy-start.2 = (bf16[32,2,16,128]{3,2,1,0:T(8,128)(2,1)S(1)}, bf16[32,2,16,128]{3,2,1,0:T(8,128)(2,1)}, u32[]{:S(2)}) copy-start(bf16[32,2,16,128]{3,2,1,0:T(8,128)(2,1)} %param.5) | copy-start | bytes 786436
  7.2 15.2 %copy-start.6 = (bf16[3,3,3,32,32]{4,3,2,1,0:T(8,128)(2,1)S(1)}, bf16[3,3,3,32,32]{4,3,2,1,0:T(8,128)(2,1)}, u32[]{:S(2)}) copy-start(bf16[3,3,3,32,32]{4,3,2,1,0:T(8,128)(2,1)} %param.8) | copy-start | bytes 165892
  7.2 230.3 %all-reduce.7.cloned.1.call-start = ((), (), s32[]{:S(2)}) async-start(), calls=%async_computation.1 | async-start | bytes 2359296 | tf_op jit(solution)/shard_map/psum | solution.py:11
  8.3 36.4 %copy-start.3 = (bf16[32,2,16,128]{3,0,2,1:T(8,128)(2,1)}, bf16[32,2,16,128]{3,0,2,1:T(8,128)(2,1)S(1)}, u32[]{:S(2)}) copy-start(bf16[32,2,16,128]{3,0,2,1:T(8,128)(2,1)S(1)} %copy.134) | copy-start | bytes 786436
  8.4 10.7 %collective-permute-start.1 = (bf16[32,1,16,128]{3,0,2,1:T(8,128)(2,1)S(1)}, bf16[32,1,16,128]{3,0,2,1:T(8,128)(2,1)S(1)}, u32[]{:S(2)}, u32[]{:S(2)}) collective-permute-start(bf16[32,1,16,128]{3,0,2,1:T(8,128)(2,1)S(1)} %get-tuple-element.142), channel_id=1, source_target_pairs={{64,0},{128,64},{192,128},{65,1},{129,65},{193,129},{66,2},{130,66... | collective-permute-start | bytes 393224 | tf_op jit(solution)/shard_map/ppermute | solution.py:28
  12.1 6.9 collective-permute-start
  19.0 23.4 %copy-start.61 = (bf16[32,1,16,128]{3,0,2,1:T(8,128)(2,1)}, bf16[32,1,16,128]{3,0,2,1:T(8,128)(2,1)S(1)}, u32[]{:S(2)}) copy-start(bf16[32,1,16,128]{3,0,2,1:T(8,128)(2,1)S(1)} %collective-permute-done) | copy-start | bytes 393220
  19.1 25.7 %copy-start.59 = (bf16[32,1,16,128]{3,0,2,1:T(8,128)(2,1)}, bf16[32,1,16,128]{3,0,2,1:T(8,128)(2,1)S(1)}, u32[]{:S(2)}) copy-start(bf16[32,1,16,128]{3,0,2,1:T(8,128)(2,1)S(1)} %collective-permute-done.1) | copy-start | bytes 393220
  19.2 3.9 collective-permute-start.2
  21.0 5.8 collective-permute-start.3
  28.8 5.9 collective-permute-start.5
  30.1 4.1 collective-permute-start.4
  33.2 10.9 %copy-start.23 = (bf16[32,2,16,128]{3,0,2,1:T(8,128)(2,1)}, bf16[32,2,16,128]{3,0,2,1:T(8,128)(2,1)S(1)}, u32[]{:S(2)}) copy-start(bf16[32,2,16,128]{3,0,2,1:T(8,128)(2,1)S(1)} %get-tuple-element.126) | copy-start | bytes 786436
  45.7 10.8 %collective-permute-start.6 = (bf16[2,32,1,16,128]{4,1,3,2,0:T(8,128)(2,1)S(1)}, bf16[2,32,1,16,128]{4,1,3,2,0:T(8,128)(2,1)S(1)}, u32[]{:S(2)}, u32[]{:S(2)}) collective-permute-start(bf16[2,32,1,16,128]{4,1,3,2,0:T(8,128)(2,1)S(1)} %get-tuple-element.134), channel_id=1, source_target_pairs={{0,64},{64,128},{128,192},{1,65},{65,129},{129,193},{2,66},{66,130... | collective-permute-start | bytes 786440 | tf_op jit(solution)/shard_map/ppermute | solution.py:26
  49.5 11.1 %collective-permute-start.7 = (bf16[2,32,1,16,128]{4,1,3,2,0:T(8,128)(2,1)S(1)}, bf16[2,32,1,16,128]{4,1,3,2,0:T(8,128)(2,1)S(1)}, u32[]{:S(2)}, u32[]{:S(2)}) collective-permute-start(bf16[2,32,1,16,128]{4,1,3,2,0:T(8,128)(2,1)S(1)} %get-tuple-element.135), channel_id=1, source_target_pairs={{64,0},{128,64},{192,128},{65,1},{129,65},{193,129},{66,2},{130,66... | collective-permute-start | bytes 786440 | tf_op jit(solution)/shard_map/ppermute | solution.py:28
  56.5 16.9 %copy-start = (bf16[2,32,1,16,128]{4,1,3,2,0:T(8,128)(2,1)}, bf16[2,32,1,16,128]{4,1,3,2,0:T(8,128)(2,1)S(1)}, u32[]{:S(2)}) copy-start(bf16[2,32,1,16,128]{4,1,3,2,0:T(8,128)(2,1)S(1)} %collective-permute-done.6) | copy-start | bytes 786436
  60.6 12.8 %copy-start.1 = (bf16[2,32,1,16,128]{4,1,3,2,0:T(8,128)(2,1)}, bf16[2,32,1,16,128]{4,1,3,2,0:T(8,128)(2,1)S(1)}, u32[]{:S(2)}) copy-start(bf16[2,32,1,16,128]{4,1,3,2,0:T(8,128)(2,1)S(1)} %collective-permute-done.7) | copy-start | bytes 786436
  60.6 5.4 collective-permute-start.8
  64.0 9.4 collective-permute-start.9
  76.4 10.8 %copy-start.65 = (bf16[1,1,3,32,32]{3,4,2,1,0:T(8,128)(2,1)S(1)}, bf16[1,1,3,32,32]{3,4,2,1,0:T(8,128)(2,1)}, u32[]{:S(2)}) copy-start(bf16[1,1,3,32,32]{3,4,2,1,0:T(8,128)(2,1)} %get-tuple-element.151) | copy-start | bytes 18436
  76.4 11.5 %copy-start.64 = (bf16[1,1,3,32,32]{3,4,2,1,0:T(8,128)(2,1)S(1)}, bf16[1,1,3,32,32]{3,4,2,1,0:T(8,128)(2,1)}, u32[]{:S(2)}) copy-start(bf16[1,1,3,32,32]{3,4,2,1,0:T(8,128)(2,1)} %get-tuple-element.152) | copy-start | bytes 18436
  77.3 12.3 %collective-permute-start.11 = (bf16[2,32,4,18,1]{1,2,4,3,0:T(4,128)(2,1)S(1)}, bf16[2,32,4,18,1]{1,2,4,3,0:T(4,128)(2,1)}, u32[]{:S(2)}, u32[]{:S(2)}) collective-permute-start(bf16[2,32,4,18,1]{1,2,4,3,0:T(4,128)(2,1)S(1)} %copy.163), channel_id=1, source_target_pairs={{1,0},{2,1},{3,2},{4,3},{5,4},{6,5},{7,6},{9,8},{10,9},{11,10},{12... | collective-permute-start | bytes 27656 | tf_op jit(solution)/shard_map/ppermute | solution.py:28
  78.6 10.0 collective-permute-start.10
  109.9 8.0 collective-permute-start.12
  112.8 8.2 collective-permute-start.13
  121.0 12.4 %collective-permute-start.14 = (bf16[32,4,1,128]{3,0,2,1:T(8,128)(2,1)S(1)}, bf16[32,4,1,128]{3,0,2,1:T(8,128)(2,1)S(1)}, u32[]{:S(2)}, u32[]{:S(2)}) collective-permute-start(bf16[32,4,1,128]{3,0,2,1:T(8,128)(2,1)S(1)} %get-tuple-element.132), channel_id=1, source_target_pairs={{0,8},{8,16},{16,24},{24,32},{32,40},{40,48},{48,56},{1,9},{9,17},... | collective-permute-start | bytes 98312 | tf_op jit(solution)/shard_map/ppermute | solution.py:26
  131.0 5.8 collective-permute-start.15
  138.1 6.0 collective-permute-start.17
  139.4 4.2 collective-permute-start.16
  162.1 75.4 %copy-start.7 = (bf16[3,3,3,32,32]{4,3,2,1,0:T(8,128)(2,1)S(1)}, bf16[3,3,3,32,32]{4,3,2,1,0:T(8,128)(2,1)}, u32[]{:S(2)}) copy-start(bf16[3,3,3,32,32]{4,3,2,1,0:T(8,128)(2,1)} %param.8) | copy-start | bytes 165892
  163.1 74.6 %copy-start.8 = (bf16[3,3,3,32,32]{4,3,2,1,0:T(8,128)(2,1)S(1)}, bf16[3,3,3,32,32]{4,3,2,1,0:T(8,128)(2,1)}, u32[]{:S(2)}) copy-start(bf16[3,3,3,32,32]{4,3,2,1,0:T(8,128)(2,1)} %param.9) | copy-start | bytes 165892
  163.2 848.0 %all-reduce.5.cloned.1.call-start = ((), (), s32[]{:S(2)}) async-start(), calls=%async_computation | async-start | bytes 2359296 | tf_op jit(solution)/shard_map/psum | solution.py:12
  (95 other events, 257.1 us)
Sparse Core Ops, SparseCore 0:
  163.3 74.1 all-reduce.6
  240.2 770.8 all-reduce.4
